TPU v7x, 16 devices: a whole 2x2x2 slice. The times are simulated.
16 devices in a mesh: data: 4 (over z, y), tp: 4 (over x, core).
Axes of the slice: x: 2, y: 2, z: 2, core: 2. Of those that a mesh axis runs over, the one named last changes fastest.
Arguments:
- attn_out: bfloat16 [1024, 8192], P('data', 'tp'), parts along dimension 0
- w_out: bfloat16 [8192, 8192], P('tp')
- residual: bfloat16 [1024, 8192], P('data', 'tp'), parts along dimension 0
- norm_gain: float32 [8192], P('tp')
Outputs:
- output 1: bfloat16 [1024, 8192], P('data', 'tp'), parts along dimension 0
- output 2: bfloat16 [1024, 8192], P('data', 'tp'), parts along dimension 0
There are 4 independent parts. A program takes and returns all parts, laid end to end along the dimension named above; an argument that names none is the same for every part.
All inputs are finite; a program needn't handle non-finite values.
Results may differ from a plain program's by a relative error of at most 0.00644529.
Values are sent between devices in bfloat16 or wider.
A program may use at most 1 GiB of HBM per device.

v0:
```python
import jax
import jax.numpy as jnp
from jax import lax
from jax.sharding import PartitionSpec as P, NamedSharding

EPS = 1e-5


def solution(mesh):
    tp_size = mesh.shape["tp"]

    def local_step(attn_blk, w_blk, resid_blk, gain_blk):
        tok_rows = attn_blk.shape[0]
        d_local = resid_blk.shape[1]
        d_model = d_local * tp_size
        partial = jnp.dot(attn_blk, w_blk, preferred_element_type=jnp.float32).astype(jnp.bfloat16)
        received = lax.all_to_all(partial, "tp", 1, 0, tiled=True)
        projected = jnp.sum(received.reshape(tp_size, tok_rows, d_local), axis=0, dtype=jnp.float32)
        hidden = resid_blk.astype(jnp.float32) + projected
        sq_part = jnp.sum(hidden * hidden, axis=-1, keepdims=True)
        sq_total = lax.psum(sq_part, "tp")
        normed = hidden * lax.rsqrt(sq_total / d_model + EPS) * gain_blk
        return hidden.astype(jnp.bfloat16), normed.astype(jnp.bfloat16)

    return jax.shard_map(
        local_step,
        mesh=mesh,
        in_specs=(P("data", "tp"), P("tp", None), P("data", "tp"), P("tp")),
        out_specs=(P("data", "tp"), P("data", "tp")),
        check_vma=False,
    )
```

profile of v0, /device:TPU:0, one launch (start us, length us, event | category | flops | bytes accessed | tf_op | source)
XLA Modules:
  0.0 80.2 jit_solution(3449106275347510593)
XLA Ops:
  0.6 0.0 copy-start
  0.6 1.2 %copy-done = bf16[256,2048]{1,0:T(8,128)(2,1)S(1)} copy-done((bf16[256,2048]{1,0:T(8,128)(2,1)S(1)}, bf16[256,2048]{1,0:T(8,128)(2,1)}, u32[]{:S(2)}) %copy-start) | copy-done | bytes 1048600
  1.9 15.1 %convolution_convert_fusion = bf16[256,8192]{1,0:T(8,128)(2,1)S(1)} fusion(bf16[256,2048]{1,0:T(8,128)(2,1)S(1)} %copy-done, bf16[2048,8192]{1,0:T(8,128)(2,1)} %param.5), kind=kOutput, calls=%fused_computation | convolution fusion | flops 8592031744 | bytes 38797312 | tf_op jit(solution)/shard_map/dot_general | solution.py:16
  16.9 0.5 copy.9
  17.4 52.4 %all_to_all.13 = bf16[256,4,2048]{2,0,1:T(8,128)(2,1)S(1)} all-to-all(bf16[256,4,2048]{2,0,1:T(8,128)(2,1)S(1)} %bitcast.8), channel_id=1, replica_groups=mesh['data'=4,'tp'=4] {'tp'}, dimensions={1} | all-to-all | bytes 8388608 | tf_op jit(solution)/shard_map/all_to_all | solution.py:17
  69.9 0.0 copy-start.1
  69.9 0.8 convert_reduce_fusion
  70.7 0.4 copy-done.1
  71.1 0.0 copy-start.2
  71.1 0.4 multiply_reduce_fusion
  71.5 5.8 %psum.7 = f32[256,1]{0,1:T(1,128)S(1)} all-reduce(f32[256,1]{0,1:T(1,128)S(1)} %bitcast.10), channel_id=1, replica_groups=mesh['data'=4,'tp'=4] {'tp'}, use_global_device_ids=true, to_apply=%region_2.0 | all-reduce | flops 256 | bytes 2048 | tf_op jit(solution)/shard_map/psum | solution.py:21
  77.3 0.0 copy-done.2
  77.3 2.9 %multiply_convert_fusion = (bf16[256,2048]{1,0:T(8,128)(2,1)}, bf16[256,2048]{1,0:T(8,128)(2,1)}) fusion(f32[2048]{0:T(1024)S(1)} %copy-done.2, f32[256]{0:T(256)S(1)} %bitcast.11, f32[256,2048]{1,0:T(8,128)S(1)} %convert_reduce_fusion, bf16[256,2048]{1,0:T(8,128)(2,1)} %param.6), kind=kLoop, calls=%fused_computation.3 | loop fusion | flops 3145728 | bytes 5252096 | tf_op jit(solution)/shard_map/convert_element_type | solution.py:23
  (1 shorter events, 0.0 us)
Async XLA Ops:
  0.6 1.2 %copy-start = (bf16[256,2048]{1,0:T(8,128)(2,1)S(1)}, bf16[256,2048]{1,0:T(8,128)(2,1)}, u32[]{:S(2)}) copy-start(bf16[256,2048]{1,0:T(8,128)(2,1)} %param.4) | copy-start | bytes 3145732
  69.9 1.2 %copy-start.1 = (bf16[256,2048]{1,0:T(8,128)(2,1)S(1)}, bf16[256,2048]{1,0:T(8,128)(2,1)}, u32[]{:S(2)}) copy-start(bf16[256,2048]{1,0:T(8,128)(2,1)} %param.6) | copy-start | bytes 3145732
  71.1 6.2 %copy-start.2 = (f32[2048]{0:T(1024)S(1)}, f32[2048]{0:T(1024)}, u32[]{:S(2)}) copy-start(f32[2048]{0:T(1024)} %param.7) | copy-start | bytes 24580
where the time goes:
time: 80.5 us; the launch traced here: 80.2 us
  blocking collectives  58.2 us (72%)
  matrix products  15.1 us (19%)
  other arithmetic  4.1 us (5%)
  local copies, waits for them, and re-layouts  2.15 us (3%)
    all_to_all x1, blocking collectives, local_step(): received = lax.all_to_all(partial, 'tp', 1, 0, tiled=True)  52.4 us
    dot_general x1, matrix products, local_step(): jnp.dot(attn_blk, w_blk, preferred_element_type=jnp.float32)  15.1 us
    psum x1, blocking collectives, local_step(): sq_total = lax.psum(sq_part, 'tp')  5.76 us
    convert_element_type x1, other arithmetic, local_step(): return (hidden.astype(jnp.bfloat16), normed.astype(jnp.bfloat16))  2.89 us
    unnamed x6, local copies, waits for them, and re-layouts  1.64 us

commit v1 on v0

v1 whole, which is shorter than its diff:
```python
import functools

import jax
import jax.numpy as jnp
from jax import lax
from jax.experimental import pallas as pl
from jax.experimental.pallas import tpu as pltpu
from jax.sharding import PartitionSpec as P

EPS = 1e-5
CN = 256
RB = 128
DEPTH = 6
LANES = 128
MESH = pl.DeviceIdType.MESH


def kernel(n_tp, a_hbm, w_hbm, r_hbm, g_hbm, hid_ref, nrm_ref,
           a, w, res, gain, sbuf, pbuf, own, rbuf, sq, st_out, st_in,
           a_sem, w_sem, r_sem, g_sem, ss_sem, sp_sem, rr_sem, rp_sem, sst_sem, rst_sem):
    rows, d_local = hid_ref.shape
    d_model = d_local * n_tp
    nch = d_local // CN
    nrb = rows // RB
    half = 2 * nch
    total = 4 * nch

    me = lax.axis_index("tp")
    chip = me // 2
    core = me % 2
    partner = chip * 2 + (1 - core)
    far = (1 - chip) * 2

    def dev(t):
        return {"tp": t}

    def owner_chunk(i):
        if isinstance(i, int):
            if i < half:
                return far + i % 2, i // 2
            if i < half + nch:
                return partner, i - half
            return me, i - half - nch
        is_far = jnp.int32(i < half)
        is_part = jnp.int32(i < half + nch) - is_far
        is_own = 1 - is_far - is_part
        o = is_far * (far + i % 2) + is_part * partner + is_own * me
        c = is_far * (i // 2) + is_part * (i - half) + is_own * (i - half - nch)
        return o, c

    def w_copy(i):
        o, c = owner_chunk(i)
        col = pl.multiple_of(o * d_local + c * CN, CN)
        return pltpu.make_async_copy(w_hbm.at[:, pl.ds(col, CN)], w.at[i], w_sem.at[i])

    a_copy = pltpu.make_async_copy(a_hbm, a, a_sem)
    a_copy.start()
    for i in range(DEPTH):
        w_copy(i).start()
    r_copy = pltpu.make_async_copy(r_hbm, res, r_sem)
    r_copy.start()
    g_copy = pltpu.make_async_copy(g_hbm, gain, g_sem)
    g_copy.start()

    barrier = pltpu.get_barrier_semaphore()
    for k in range(1, n_tp):
        pl.semaphore_signal(barrier, inc=1, device_id=dev((me + k) % n_tp), device_id_type=MESH)

    def product(i):
        @pl.when(i + DEPTH < total)
        def _():
            w_copy(i + DEPTH).start()

        w_copy(i).wait()
        return jnp.dot(a[...], w[i], preferred_element_type=jnp.float32)

    def far_send(i, b):
        src = sbuf.at[i, pl.ds(b * RB, RB), :]
        dst = rbuf.at[1 + core, i // 2, pl.ds(b * RB, RB), :]
        return pltpu.make_async_remote_copy(
            src_ref=src, dst_ref=dst, send_sem=ss_sem.at[i, b], recv_sem=rr_sem.at[core, i // 2, b],
            device_id=dev(far + i % 2), device_id_type=MESH)

    def far_recv(s, c, b):
        ref = rbuf.at[1 + s, c, pl.ds(b * RB, RB), :]
        return pltpu.make_async_remote_copy(
            src_ref=ref, dst_ref=ref, send_sem=ss_sem.at[c, b], recv_sem=rr_sem.at[s, c, b],
            device_id=dev(partner), device_id_type=MESH)

    def part_send(c):
        return pltpu.make_async_remote_copy(
            src_ref=pbuf.at[c], dst_ref=rbuf.at[0, c], send_sem=sp_sem.at[c], recv_sem=rp_sem.at[c],
            device_id=dev(partner), device_id_type=MESH)

    a_copy.wait()
    pl.semaphore_wait(barrier, n_tp - 1)

    @pl.loop(0, half)
    def _(i):
        sbuf[i] = product(i).astype(jnp.bfloat16)
        far_send(i, 0).start()

    for b in range(1, nrb):
        @pl.loop(0, half)
        def _(i):
            far_send(i, b).start()

    @pl.loop(0, nch)
    def _(c):
        pbuf[c] = product(half + c).astype(jnp.bfloat16)
        part_send(c).start()

    r_copy.wait()
    g_copy.wait()

    @pl.loop(0, nch)
    def _(c):
        cols = pl.ds(pl.multiple_of(c * CN, CN), CN)
        own[c] = product(half + nch + c) + res[:, cols].astype(jnp.float32)

    @pl.loop(0, nch)
    def _(c):
        part_send(c).wait_recv()
        own[c] = own[c] + rbuf[0, c].astype(jnp.float32)

    def add_block(b, lo, hi):
        rs = pl.ds(b * RB, RB)

        @pl.loop(lo, hi)
        def _(c):
            cols = pl.ds(pl.multiple_of(c * CN, CN), CN)
            far_recv(0, c, b).wait_recv()
            far_recv(1, c, b).wait_recv()
            h = own[c, rs, :] + (rbuf[1, c, rs, :].astype(jnp.float32) + rbuf[2, c, rs, :].astype(jnp.float32))
            own[c, rs, :] = h
            hid_ref[rs, cols] = h.astype(jnp.bfloat16)
            h2 = h * h
            s = h2[:, :LANES]
            for k in range(1, CN // LANES):
                s = s + h2[:, k * LANES:(k + 1) * LANES]
            sq[b] = sq[b] + s

    def stat_copy(b, k):
        return pltpu.make_async_remote_copy(
            src_ref=st_out.at[b], dst_ref=st_in.at[b, k - 1], send_sem=sst_sem.at[b, k - 1],
            recv_sem=rst_sem.at[b, k - 1], device_id=dev((me + k) % n_tp), device_id_type=MESH)

    def send_stats(b):
        t = jnp.sum(sq[b].T, axis=0, keepdims=True)
        st_out[b] = jnp.broadcast_to(t, (8, RB))
        for k in range(1, n_tp):
            stat_copy(b, k).start()

    def normalise(b):
        rs = pl.ds(b * RB, RB)
        for k in range(1, n_tp):
            stat_copy(b, k).wait_recv()
        t = st_out[b] + st_in[b, 0] + st_in[b, 1] + st_in[b, 2]
        inv = lax.rsqrt(t / d_model + EPS)
        sq[b] = jnp.broadcast_to(inv[0:1], (LANES, RB)).T

        @pl.loop(0, nch)
        def _(c):
            for k in range(CN // LANES):
                cols = pl.ds(pl.multiple_of(c * CN + k * LANES, LANES), LANES)
                v = own[c, rs, k * LANES:(k + 1) * LANES] * sq[b] * gain[:, cols]
                nrm_ref[rs, cols] = v.astype(jnp.bfloat16)

    sq[...] = jnp.zeros_like(sq)
    for b in range(nrb):
        if b == 0:
            add_block(b, 0, nch)
        else:
            add_block(b, 0, nch // 2)
            normalise(b - 1)
            add_block(b, nch // 2, nch)
        send_stats(b)
    normalise(nrb - 1)

    @pl.loop(0, half)
    def _(i):
        for b in range(nrb):
            far_send(i, b).wait_send()

    @pl.loop(0, nch)
    def _(c):
        part_send(c).wait_send()

    for b in range(nrb):
        for k in range(1, n_tp):
            stat_copy(b, k).wait_send()


def solution(mesh):
    n_tp = mesh.shape["tp"]

    def local_step(attn_blk, w_blk, resid_blk, gain_blk):
        rows, depth = attn_blk.shape
        d_local = resid_blk.shape[1]
        nch = d_local // CN
        nrb = rows // RB
        out = jax.ShapeDtypeStruct((rows, d_local), jnp.bfloat16)
        bf, f32 = jnp.bfloat16, jnp.float32
        dma = pltpu.SemaphoreType.DMA
        return pl.pallas_call(
            functools.partial(kernel, n_tp),
            out_shape=(out, out),
            in_specs=[pl.BlockSpec(memory_space=pl.ANY)] * 4,
            out_specs=(pl.BlockSpec(memory_space=pltpu.VMEM),) * 2,
            scratch_shapes=[
                pltpu.VMEM((rows, depth), bf),
                pltpu.VMEM((4 * nch, depth, CN), bf),
                pltpu.VMEM((rows, d_local), bf),
                pltpu.VMEM((1, d_local), f32),
                pltpu.VMEM((2 * nch, rows, CN), bf),
                pltpu.VMEM((nch, rows, CN), bf),
                pltpu.VMEM((nch, rows, CN), f32),
                pltpu.VMEM((3, nch, rows, CN), bf),
                pltpu.VMEM((nrb, RB, LANES), f32),
                pltpu.VMEM((nrb, 8, RB), f32),
                pltpu.VMEM((nrb, n_tp - 1, 8, RB), f32),
                dma, dma((4 * nch,)), dma, dma,
                dma((2 * nch, nrb)), dma((nch,)),
                dma((2, nch, nrb)), dma((nch,)),
                dma((nrb, n_tp - 1)), dma((nrb, n_tp - 1)),
            ],
            compiler_params=pltpu.CompilerParams(
                collective_id=0, has_side_effects=True, vmem_limit_bytes=56 * 1024 * 1024),
        )(attn_blk, w_blk, resid_blk, gain_blk.reshape(1, d_local))

    return jax.shard_map(
        local_step,
        mesh=mesh,
        in_specs=(P("data", "tp"), P("tp", None), P("data", "tp"), P("tp")),
        out_specs=(P("data", "tp"), P("data", "tp")),
        check_vma=False,
    )
```

time: 80.5 us -> 62.6 us (0.78)
  blocking collectives: 58.2 us -> 0 us
  Pallas kernels: 0 us -> 57.2 us
  matrix products: 15.1 us -> 0 us
  other arithmetic: 4.1 us -> 0 us
  local copies, waits for them, and re-layouts: 2.15 us -> 4.61 us
    pallas_call x0 -> x1, Pallas kernels: none -> 57.2 us  [local_step(): pl.pallas_call(functools.partial(kernel, n_tp), out_shape=(out, out), in_...]
    all_to_all x1 -> x0, blocking collectives: 52.4 us -> none  [local_step(): received = lax.all_to_all(partial, 'tp', 1, 0, tiled=True)]
    dot_general x1 -> x0, matrix products: 15.1 us -> none  [local_step(): jnp.dot(attn_blk, w_blk, preferred_element_type=jnp.float32)]
    psum x1 -> x0, blocking collectives: 5.76 us -> none  [local_step(): sq_total = lax.psum(sq_part, 'tp')]
    unnamed x6 -> x2, local copies, waits for them, and re-layouts: 1.64 us -> 4.61 us
    convert_element_type x1 -> x0, other arithmetic: 2.89 us -> none  [local_step(): return (hidden.astype(jnp.bfloat16), normed.astype(jnp.bfloat16))]
    reduce_sum x2 -> x0, other arithmetic: 1.2 us -> none  [the longest x1 0.8 us: local_step(): jnp.sum(received.reshape(tp_size, tok_rows, d_local), axis=0, dtype=jnp.f...]
where the time goes in v1:
time: 62.6 us; the launch traced here: 62.4 us
  Pallas kernels  57.2 us (91%)
  local copies, waits for them, and re-layouts  4.61 us (7%)
  between operations  0.64 us (1%)
    pallas_call x1, Pallas kernels, local_step(): pl.pallas_call(functools.partial(kernel, n_tp), out_shape=(out, out), in_...  57.2 us
    unnamed x2, local copies, waits for them, and re-layouts  4.61 us

profile of v1, /device:TPU:0, one launch (start us, length us, event | category | flops | bytes accessed | tf_op | source)
XLA Modules:
  0.0 62.4 jit_solution(2099730212841584150)
XLA Ops:
  0.6 57.2 %shard_map.59 = (bf16[256,2048]{1,0:T(8,128)(2,1)}, bf16[256,2048]{1,0:T(8,128)(2,1)}) custom-call(bf16[256,2048]{1,0:T(8,128)(2,1)} %a_hbm.1, bf16[2048,8192]{1,0:T(8,128)(2,1)} %w_hbm.1, bf16[256,2048]{1,0:T(8,128)(2,1)} %r_hbm.1, f32[1,2048]{1,0:T(1,128)} %bitcast.1), custom_call_target="tpu_custom_call" | custom-call | tf_op jit(solution)/shard_map/pallas_call | solution.py:205
  57.8 2.3 %copy.8 = bf16[256,2048]{1,0:T(8,128)(2,1)} copy(bf16[256,2048]{1,0:T(8,128)(2,1)} %get-tuple-element.4) | data formatting | bytes 2097152
  60.1 2.3 %copy.9 = bf16[256,2048]{1,0:T(8,128)(2,1)} copy(bf16[256,2048]{1,0:T(8,128)(2,1)} %get-tuple-element.5) | data formatting | bytes 2097152

commit v2 on v1

--- a/solution.py
+++ b/solution.py
@@ -92,12 +92,15 @@
             src_ref=pbuf.at[c], dst_ref=rbuf.at[0, c], send_sem=sp_sem.at[c], recv_sem=rp_sem.at[c],
             device_id=dev(partner), device_id_type=MESH)
 
-    a_copy.wait()
-    pl.semaphore_wait(barrier, n_tp - 1)
+    with jax.named_scope("a_wait"):
+        a_copy.wait()
+    with jax.named_scope("barrier_wait"):
+        pl.semaphore_wait(barrier, n_tp - 1)
 
     @pl.loop(0, half)
     def _(i):
-        sbuf[i] = product(i).astype(jnp.bfloat16)
+        with jax.named_scope("far_product"):
+            sbuf[i] = product(i).astype(jnp.bfloat16)
         far_send(i, 0).start()
 
     for b in range(1, nrb):
@@ -107,7 +110,8 @@
 
     @pl.loop(0, nch)
     def _(c):
-        pbuf[c] = product(half + c).astype(jnp.bfloat16)
+        with jax.named_scope("part_product"):
+            pbuf[c] = product(half + c).astype(jnp.bfloat16)
         part_send(c).start()
 
     r_copy.wait()
@@ -116,7 +120,8 @@
     @pl.loop(0, nch)
     def _(c):
         cols = pl.ds(pl.multiple_of(c * CN, CN), CN)
-        own[c] = product(half + nch + c) + res[:, cols].astype(jnp.float32)
+        with jax.named_scope("own_product"):
+            own[c] = product(half + nch + c) + res[:, cols].astype(jnp.float32)
 
     @pl.loop(0, nch)
     def _(c):
@@ -129,8 +134,9 @@
         @pl.loop(lo, hi)
         def _(c):
             cols = pl.ds(pl.multiple_of(c * CN, CN), CN)
-            far_recv(0, c, b).wait_recv()
-            far_recv(1, c, b).wait_recv()
+            with jax.named_scope(f"far_wait{b}"):
+                far_recv(0, c, b).wait_recv()
+                far_recv(1, c, b).wait_recv()
             h = own[c, rs, :] + (rbuf[1, c, rs, :].astype(jnp.float32) + rbuf[2, c, rs, :].astype(jnp.float32))
             own[c, rs, :] = h
             hid_ref[rs, cols] = h.astype(jnp.bfloat16)
@@ -146,15 +152,17 @@
             recv_sem=rst_sem.at[b, k - 1], device_id=dev((me + k) % n_tp), device_id_type=MESH)
 
     def send_stats(b):
-        t = jnp.sum(sq[b].T, axis=0, keepdims=True)
-        st_out[b] = jnp.broadcast_to(t, (8, RB))
-        for k in range(1, n_tp):
-            stat_copy(b, k).start()
+        with jax.named_scope(f"send_stats{b}"):
+            t = jnp.sum(sq[b].T, axis=0, keepdims=True)
+            st_out[b] = jnp.broadcast_to(t, (8, RB))
+            for k in range(1, n_tp):
+                stat_copy(b, k).start()
 
     def normalise(b):
         rs = pl.ds(b * RB, RB)
-        for k in range(1, n_tp):
-            stat_copy(b, k).wait_recv()
+        with jax.named_scope(f"stat_wait{b}"):
+            for k in range(1, n_tp):
+                stat_copy(b, k).wait_recv()
         t = st_out[b] + st_in[b, 0] + st_in[b, 1] + st_in[b, 2]
         inv = lax.rsqrt(t / d_model + EPS)
         sq[b] = jnp.broadcast_to(inv[0:1], (LANES, RB)).T
@@ -177,10 +185,11 @@
         send_stats(b)
     normalise(nrb - 1)
 
-    @pl.loop(0, half)
-    def _(i):
-        for b in range(nrb):
-            far_send(i, b).wait_send()
+    with jax.named_scope("drain"):
+        @pl.loop(0, half)
+        def _(i):
+            for b in range(nrb):
+                far_send(i, b).wait_send()
 
     @pl.loop(0, nch)
     def _(c):
@@ -199,7 +208,7 @@
         d_local = resid_blk.shape[1]
         nch = d_local // CN
         nrb = rows // RB
-        out = jax.ShapeDtypeStruct((rows, d_local), jnp.bfloat16)
+        out = pltpu.VMEM((rows, d_local), jnp.bfloat16)
         bf, f32 = jnp.bfloat16, jnp.float32
         dma = pltpu.SemaphoreType.DMA
         return pl.pallas_call(

time: 62.6 us -> 58.5 us (0.935)
  local copies, waits for them, and re-layouts: 4.61 us -> 1.94 us
  Pallas kernels: 57.2 us -> 55.8 us
    unnamed x2, local copies, waits for them, and re-layouts: 4.61 us -> 1.94 us
    pallas_call x1, Pallas kernels: 57.2 us -> 55.8 us  [local_step(): pl.pallas_call(functools.partial(kernel, n_tp), out_shape=(out, out), in_...]
where the time goes in v2:
time: 58.5 us; the launch traced here: 58.4 us
  Pallas kernels  55.8 us (95%)
  local copies, waits for them, and re-layouts  1.94 us (3%)
  between operations  0.64 us (1%)
    pallas_call x1, Pallas kernels, local_step(): pl.pallas_call(functools.partial(kernel, n_tp), out_shape=(out, out), in_...  55.8 us
    unnamed x2, local copies, waits for them, and re-layouts  1.94 us

profile of v2, /device:TPU:0, one launch (start us, length us, event | category | flops | bytes accessed | tf_op | source)
XLA Modules:
  0.0 58.4 jit_solution(6136205249270984772)
XLA Ops:
  0.6 55.8 %shard_map.59 = (bf16[256,2048]{1,0:T(8,128)(2,1)S(1)}, bf16[256,2048]{1,0:T(8,128)(2,1)S(1)}) custom-call(bf16[256,2048]{1,0:T(8,128)(2,1)} %a_hbm.1, bf16[2048,8192]{1,0:T(8,128)(2,1)} %w_hbm.1, bf16[256,2048]{1,0:T(8,128)(2,1)} %r_hbm.1, f32[1,2048]{1,0:T(1,128)} %bitcast.1), custom_call_target="tpu_custom_call" | custom-call | tf_op jit(solution)/shard_map/pallas_call | solution.py:214
  56.4 1.0 %copy.8 = bf16[256,2048]{1,0:T(8,128)(2,1)} copy(bf16[256,2048]{1,0:T(8,128)(2,1)S(1)} %get-tuple-element.2) | data formatting | bytes 2097152
  57.4 1.0 %copy.9 = bf16[256,2048]{1,0:T(8,128)(2,1)} copy(bf16[256,2048]{1,0:T(8,128)(2,1)S(1)} %get-tuple-element.3) | data formatting | bytes 2097152

commit v3 on v2

v3 whole, which is shorter than its diff:
```python
import functools

import jax
import jax.numpy as jnp
from jax import lax
from jax.experimental import pallas as pl
from jax.experimental.pallas import tpu as pltpu
from jax.sharding import PartitionSpec as P

EPS = 1e-5
CN = 256
RB = 128
DEPTH = 6
WSEM = 8
LEAD = 3
LANES = 128
MESH = pl.DeviceIdType.MESH


def fold(x):
    s = x[:, :LANES]
    for k in range(1, x.shape[1] // LANES):
        s = s + x[:, k * LANES:(k + 1) * LANES]
    return s


def main_kernel(n_tp, a_hbm, w_hbm, r_hbm, g_hbm,
                hid_ref, nrm_ref, last_ref, scale_ref, gain,
                a, w, res, sbuf, pbuf, own, rbuf, sq, st_out, st_in,
                a_sem, w_sem, r_sem, g_sem, ss_sem, sp_sem, rr_sem, rp_sem, sst_sem, rst_sem):
    rows, d_local = hid_ref.shape
    d_model = d_local * n_tp
    nch = d_local // CN
    nrb = rows // RB
    half = 2 * nch
    total = 4 * nch
    last = nrb - 1

    me = lax.axis_index("tp")
    chip = me // 2
    core = me % 2
    partner = chip * 2 + (1 - core)
    far = (1 - chip) * 2

    def dev(t):
        return {"tp": t}

    def block(b):
        return pl.ds(b * RB, RB)

    def w_copy(i):
        if isinstance(i, int):
            i = jnp.int32(i)
        is_far = jnp.int32(i < half)
        is_part = jnp.int32(i < half + nch) - is_far
        is_own = 1 - is_far - is_part
        o = is_far * (far + i % 2) + is_part * partner + is_own * me
        c = is_far * (i // 2) + is_part * (i - half) + is_own * (i - half - nch)
        col = pl.multiple_of(o * d_local + c * CN, CN)
        return pltpu.make_async_copy(w_hbm.at[:, pl.ds(col, CN)], w.at[i], w_sem.at[i % WSEM])

    def a_copy(k):
        rs = pl.ds(k * (rows // 2), rows // 2)
        return pltpu.make_async_copy(a_hbm.at[rs], a.at[rs], a_sem.at[k])

    a_copy(0).start()
    w_copy(0).start()
    barrier = pltpu.get_barrier_semaphore()
    for k in range(1, n_tp):
        pl.semaphore_signal(barrier, inc=1, device_id=dev((me + k) % n_tp), device_id_type=MESH)
    with jax.named_scope("barrier_wait"):
        pl.semaphore_wait(barrier, n_tp - 1)
    a_copy(1).start()
    for i in range(1, DEPTH):
        w_copy(i).start()
    r_copy = pltpu.make_async_copy(r_hbm, res, r_sem)
    g_copy = pltpu.make_async_copy(g_hbm, gain, g_sem)
    r_copy.start()
    g_copy.start()

    def product(i):
        @pl.when(i + DEPTH < total)
        def _():
            w_copy(i + DEPTH).start()

        w_copy(i).wait()
        return jnp.dot(a[...], w[i], preferred_element_type=jnp.float32)

    def far_send(i, b):
        return pltpu.make_async_remote_copy(
            src_ref=sbuf.at[i, block(b), :], dst_ref=rbuf.at[1 + core, i // 2, block(b), :],
            send_sem=ss_sem, recv_sem=rr_sem.at[i // 2, b],
            device_id=dev(far + i % 2), device_id_type=MESH)

    def local_wait(ref, sem):
        pltpu.make_async_copy(ref, ref, sem).wait()

    def part_send(c):
        return pltpu.make_async_remote_copy(
            src_ref=pbuf.at[c], dst_ref=rbuf.at[0, c], send_sem=sp_sem, recv_sem=rp_sem,
            device_id=dev(partner), device_id_type=MESH)

    with jax.named_scope("a_wait"):
        a_copy(0).wait()
    with jax.named_scope("w0_wait"):
        w_copy(0).wait()
    hr = rows // 2
    with jax.named_scope("first"):
        sbuf[0, :hr] = jnp.dot(a[:hr], w[0], preferred_element_type=jnp.float32).astype(jnp.bfloat16)
    far_send(0, 0).start()
    w_copy(DEPTH).start()
    a_copy(1).wait()

    @pl.loop(1, half)
    def _(i):
        with jax.named_scope("far_product"):
            sbuf[i] = product(i).astype(jnp.bfloat16)
        far_send(i, 0).start()

    sbuf[0, hr:] = jnp.dot(a[hr:], w[0], preferred_element_type=jnp.float32).astype(jnp.bfloat16)

    @pl.loop(0, nch)
    def _(c):
        with jax.named_scope("part_product"):
            pbuf[c] = product(half + c).astype(jnp.bfloat16)
        part_send(c).start()

    r_copy.wait()
    g_copy.wait()

    @pl.loop(0, nch)
    def _(c):
        cols = pl.ds(pl.multiple_of(c * CN, CN), CN)
        with jax.named_scope("own_product"):
            own[c] = product(half + nch + c) + res[:, cols].astype(jnp.float32)

    local_wait(rbuf.at[0], rp_sem)

    @pl.loop(0, nch)
    def _(c):
        own[c] = own[c] + rbuf[0, c].astype(jnp.float32)

    def issue(q):
        b, c = divmod(q, nch)
        if 1 <= b < nrb:
            far_send(2 * c, b).start()
            far_send(2 * c + 1, b).start()

    def add_chunk(b, c):
        cols = pl.ds(c * CN, CN)
        with jax.named_scope(f"far_wait{b}"):
            local_wait(rbuf.at[pl.ds(1, 2), c, block(b), :], rr_sem.at[c, b])
        issue(b * nch + c + LEAD)
        rs = block(b)
        h = own[c, rs, :] + (rbuf[1, c, rs, :].astype(jnp.float32) + rbuf[2, c, rs, :].astype(jnp.float32))
        hid_ref[rs, cols] = h.astype(jnp.bfloat16)
        if b == last:
            last_ref[:, cols] = h
        else:
            own[c, rs, :] = h
        s = fold(h * h)
        sq[b] = s if c == 0 else sq[b] + s

    def stat_copy(b, k):
        return pltpu.make_async_remote_copy(
            src_ref=st_out.at[b], dst_ref=st_in.at[b, k - 1], send_sem=sst_sem.at[b],
            recv_sem=rst_sem.at[b], device_id=dev((me + k) % n_tp), device_id_type=MESH)

    def send_stats(b):
        with jax.named_scope(f"send_stats{b}"):
            t = jnp.sum(sq[b].T, axis=0, keepdims=True)
            st_out[b] = jnp.broadcast_to(t, (8, RB))
            for k in range(1, n_tp):
                stat_copy(b, k).start()

    def scale(b):
        with jax.named_scope(f"stat_wait{b}"):
            local_wait(st_in.at[b], rst_sem.at[b])
        t = st_out[b] + st_in[b, 0] + st_in[b, 1] + st_in[b, 2]
        inv = lax.rsqrt(t / d_model + EPS)
        return jnp.broadcast_to(inv[0:1], (LANES, RB)).T

    def normalise(b):
        sq[b] = scale(b)

        @pl.loop(0, nch)
        def _(c):
            for k in range(CN // LANES):
                cols = pl.ds(pl.multiple_of(c * CN + k * LANES, LANES), LANES)
                v = own[c, block(b), k * LANES:(k + 1) * LANES] * sq[b] * gain[:, cols]
                nrm_ref[block(b), cols] = v.astype(jnp.bfloat16)

    for b in range(nrb):
        for c in range(nch):
            if b > 0 and c == LEAD + 2:
                normalise(b - 1)
            add_chunk(b, c)
        send_stats(b)

    with jax.named_scope("drain"):
        local_wait(sbuf, ss_sem)
        local_wait(pbuf, sp_sem)
        for b in range(last):
            local_wait(st_in.at[b], sst_sem.at[b])
    scale_ref[...] = scale(last)
    with jax.named_scope("drain2"):
        local_wait(st_in.at[last], sst_sem.at[last])


def finish_kernel(hid_ref, nrm_ref, last_ref, scale_ref, gain_ref, hid_hbm, nrm_hbm, buf, sem):
    rows, d_local = hid_hbm.shape
    early = nrm_ref.shape[0]
    late = pl.ds(early, rows - early)
    copies = [
        pltpu.make_async_copy(hid_ref, hid_hbm, sem.at[0]),
        pltpu.make_async_copy(nrm_ref, nrm_hbm.at[pl.ds(0, early)], sem.at[1]),
    ]
    for c in copies:
        c.start()

    @pl.loop(0, d_local // LANES)
    def _(j):
        cols = pl.ds(pl.multiple_of(j * LANES, LANES), LANES)
        buf[:, cols] = (last_ref[:, cols] * scale_ref[...] * gain_ref[:, cols]).astype(jnp.bfloat16)

    copies.append(pltpu.make_async_copy(buf, nrm_hbm.at[late], sem.at[2]))
    copies[-1].start()
    for c in copies:
        c.wait()


def solution(mesh):
    n_tp = mesh.shape["tp"]

    def local_step(attn_blk, w_blk, resid_blk, gain_blk):
        rows, depth = attn_blk.shape
        d_local = resid_blk.shape[1]
        nch = d_local // CN
        nrb = rows // RB
        bf, f32 = jnp.bfloat16, jnp.float32
        dma = pltpu.SemaphoreType.DMA
        vmem = pl.BlockSpec(memory_space=pltpu.VMEM)
        hbm = pl.BlockSpec(memory_space=pl.ANY)
        parts = pl.pallas_call(
            functools.partial(main_kernel, n_tp),
            out_shape=(
                pltpu.VMEM((rows, d_local), bf),
                pltpu.VMEM((rows - RB, d_local), bf),
                pltpu.VMEM((RB, d_local), f32),
                pltpu.VMEM((RB, LANES), f32),
                pltpu.VMEM((1, d_local), f32),
            ),
            in_specs=[hbm] * 4,
            out_specs=(vmem,) * 5,
            scratch_shapes=[
                pltpu.VMEM((rows, depth), bf),
                pltpu.VMEM((4 * nch, depth, CN), bf),
                pltpu.VMEM((rows, d_local), bf),
                pltpu.VMEM((2 * nch, rows, CN), bf),
                pltpu.VMEM((nch, rows, CN), bf),
                pltpu.VMEM((nch, rows, CN), f32),
                pltpu.VMEM((3, nch, rows, CN), bf),
                pltpu.VMEM((nrb, RB, LANES), f32),
                pltpu.VMEM((nrb, 8, RB), f32),
                pltpu.VMEM((nrb, n_tp - 1, 8, RB), f32),
                dma((2,)), dma((WSEM,)), dma, dma,
                dma, dma, dma((nch, nrb)), dma, dma((nrb,)), dma((nrb,)),
            ],
            compiler_params=pltpu.CompilerParams(
                collective_id=0, has_side_effects=True, vmem_limit_bytes=54 * 1024 * 1024),
        )(attn_blk, w_blk, resid_blk, gain_blk.reshape(1, d_local))
        out = jax.ShapeDtypeStruct((rows, d_local), bf)
        return pl.pallas_call(
            finish_kernel,
            out_shape=(out, out),
            in_specs=[vmem] * 5,
            out_specs=(hbm, hbm),
            scratch_shapes=[pltpu.VMEM((RB, d_local), bf), dma((3,))],
            compiler_params=pltpu.CompilerParams(vmem_limit_bytes=4 * 1024 * 1024),
        )(*parts)

    return jax.shard_map(
        local_step,
        mesh=mesh,
        in_specs=(P("data", "tp"), P("tp", None), P("data", "tp"), P("tp")),
        out_specs=(P("data", "tp"), P("data", "tp")),
        check_vma=False,
    )
```

time: 58.5 us -> 56.2 us (0.961)
  local copies, waits for them, and re-layouts: 1.94 us -> 0 us
    unnamed x2 -> x0, local copies, waits for them, and re-layouts: 1.94 us -> none
    pallas_call x1 -> x2, Pallas kernels: 55.8 us -> 55.4 us  [the longest x1 54.1 us: local_step(): pl.pallas_call(functools.partial(main_kernel, n_tp), out_shape=(pltpu.VME...]
where the time goes in v3:
time: 56.2 us; the launch traced here: 56.1 us
  Pallas kernels  55.4 us (99%)
  between operations  0.64 us (1%)
    pallas_call x1, Pallas kernels, local_step(): pl.pallas_call(functools.partial(main_kernel, n_tp), out_shape=(pltpu.VME...  54.1 us
    pallas_call x1, Pallas kernels, local_step(): pl.pallas_call(finish_kernel, out_shape=(out, out), in_specs=[vmem] * 5,...  1.34 us

profile of v3, /device:TPU:0, one launch (start us, length us, event | category | flops | bytes accessed | tf_op | source)
XLA Modules:
  0.0 56.1 jit_solution(13078529574747895219)
XLA Ops:
  0.6 54.1 %shard_map.59 = (bf16[256,2048]{1,0:T(8,128)(2,1)S(1)}, bf16[128,2048]{1,0:T(8,128)(2,1)S(1)}, f32[128,2048]{1,0:T(8,128)S(1)}, f32[128,128]{1,0:T(8,128)S(1)}, f32[1,2048]{1,0:T(1,128)S(1)}) custom-call(bf16[256,2048]{1,0:T(8,128)(2,1)} %a_hbm.1, bf16[2048,8192]{1,0:T(8,128)(2,1)} %w_hbm.1, bf16[256,2048]{1,0:T(8,128)(2,1)} %r_hbm.1, f32[1,2048]{1,0:T(1,128)} %bitcast.1), custom_call_target="tpu_custom_call" | custom-call | tf_op jit(solution)/shard_map/pallas_call | solution.py:244
  54.7 1.3 %shard_map.60 = (bf16[256,2048]{1,0:T(8,128)(2,1)}, bf16[256,2048]{1,0:T(8,128)(2,1)}) custom-call(bf16[256,2048]{1,0:T(8,128)(2,1)S(1)} %get-tuple-element.7.hid_ref, bf16[128,2048]{1,0:T(8,128)(2,1)S(1)} %get-tuple-element.8.nrm_ref, f32[128,2048]{1,0:T(8,128)S(1)} %get-tuple-element.9.last_ref, f32[128,128]{1,0:T(8,128)S(1)} %get-tuple-element.10.scale_ref, ...), custom_call_target="tpu_custom_call" | custom-call | tf_op jit(solution)/shard_map/pallas_call | solution.py:273

commit v4 on v3

--- a/solution.py
+++ b/solution.py
@@ -24,10 +24,14 @@
     return s
 
 
+def spread(inv):
+    return jnp.broadcast_to(inv[0:1], (LANES, inv.shape[1])).T
+
+
 def main_kernel(n_tp, a_hbm, w_hbm, r_hbm, g_hbm,
                 hid_ref, nrm_ref, last_ref, scale_ref, gain,
                 a, w, res, sbuf, pbuf, own, rbuf, sq, st_out, st_in,
-                a_sem, w_sem, r_sem, g_sem, ss_sem, sp_sem, rr_sem, rp_sem, sst_sem, rst_sem):
+                a_sem, w0_sem, w_sem, r_sem, g_sem, ss_sem, sp_sem, rr_sem, rp_sem, sst_sem, rst_sem):
     rows, d_local = hid_ref.shape
     d_model = d_local * n_tp
     nch = d_local // CN
@@ -63,20 +67,19 @@
         rs = pl.ds(k * (rows // 2), rows // 2)
         return pltpu.make_async_copy(a_hbm.at[rs], a.at[rs], a_sem.at[k])
 
-    a_copy(0).start()
-    w_copy(0).start()
+    def w_piece(p):
+        col = pl.multiple_of(far * d_local + p * LANES, LANES)
+        return pltpu.make_async_copy(
+            w_hbm.at[:, pl.ds(col, LANES)], w.at[0, :, pl.ds(p * LANES, LANES)], w0_sem.at[p])
+
     barrier = pltpu.get_barrier_semaphore()
     for k in range(1, n_tp):
         pl.semaphore_signal(barrier, inc=1, device_id=dev((me + k) % n_tp), device_id_type=MESH)
-    with jax.named_scope("barrier_wait"):
-        pl.semaphore_wait(barrier, n_tp - 1)
-    a_copy(1).start()
-    for i in range(1, DEPTH):
-        w_copy(i).start()
+    a_copy(0).start()
+    for p in range(CN // LANES):
+        w_piece(p).start()
     r_copy = pltpu.make_async_copy(r_hbm, res, r_sem)
     g_copy = pltpu.make_async_copy(g_hbm, gain, g_sem)
-    r_copy.start()
-    g_copy.start()
 
     def product(i):
         @pl.when(i + DEPTH < total)
@@ -102,14 +105,28 @@
 
     with jax.named_scope("a_wait"):
         a_copy(0).wait()
-    with jax.named_scope("w0_wait"):
-        w_copy(0).wait()
+    a_copy(1).start()
+    w_copy(1).start()
     hr = rows // 2
-    with jax.named_scope("first"):
-        sbuf[0, :hr] = jnp.dot(a[:hr], w[0], preferred_element_type=jnp.float32).astype(jnp.bfloat16)
-    far_send(0, 0).start()
-    w_copy(DEPTH).start()
-    a_copy(1).wait()
+    for p in range(CN // LANES):
+        cols = pl.ds(p * LANES, LANES)
+        with jax.named_scope(f"w0_wait{p}"):
+            w_piece(p).wait()
+        with jax.named_scope(f"first{p}"):
+            sbuf[0, :hr, cols] = jnp.dot(
+                a[:hr], w[0, :, cols], preferred_element_type=jnp.float32).astype(jnp.bfloat16)
+        if p == 0:
+            with jax.named_scope("barrier_wait"):
+                pl.semaphore_wait(barrier, n_tp - 1)
+        pltpu.make_async_remote_copy(
+            src_ref=sbuf.at[0, block(0), cols], dst_ref=rbuf.at[1 + core, 0, block(0), cols],
+            send_sem=ss_sem, recv_sem=rr_sem.at[0, 0], device_id=dev(far), device_id_type=MESH).start()
+    for i in range(2, DEPTH + 1):
+        w_copy(i).start()
+    r_copy.start()
+    g_copy.start()
+    with jax.named_scope("a_wait1"):
+        a_copy(1).wait()
 
     @pl.loop(1, half)
     def _(i):
@@ -177,11 +194,10 @@
         with jax.named_scope(f"stat_wait{b}"):
             local_wait(st_in.at[b], rst_sem.at[b])
         t = st_out[b] + st_in[b, 0] + st_in[b, 1] + st_in[b, 2]
-        inv = lax.rsqrt(t / d_model + EPS)
-        return jnp.broadcast_to(inv[0:1], (LANES, RB)).T
+        return lax.rsqrt(t / d_model + EPS)
 
     def normalise(b):
-        sq[b] = scale(b)
+        sq[b] = spread(scale(b))
 
         @pl.loop(0, nch)
         def _(c):
@@ -207,7 +223,7 @@
         local_wait(st_in.at[last], sst_sem.at[last])
 
 
-def finish_kernel(hid_ref, nrm_ref, last_ref, scale_ref, gain_ref, hid_hbm, nrm_hbm, buf, sem):
+def finish_kernel(hid_ref, nrm_ref, last_ref, scale_ref, gain_ref, hid_hbm, nrm_hbm, buf, scale, sem):
     rows, d_local = hid_hbm.shape
     early = nrm_ref.shape[0]
     late = pl.ds(early, rows - early)
@@ -218,10 +234,12 @@
     for c in copies:
         c.start()
 
+    scale[...] = spread(scale_ref[...])
+
     @pl.loop(0, d_local // LANES)
     def _(j):
         cols = pl.ds(pl.multiple_of(j * LANES, LANES), LANES)
-        buf[:, cols] = (last_ref[:, cols] * scale_ref[...] * gain_ref[:, cols]).astype(jnp.bfloat16)
+        buf[:, cols] = (last_ref[:, cols] * scale[...] * gain_ref[:, cols]).astype(jnp.bfloat16)
 
     copies.append(pltpu.make_async_copy(buf, nrm_hbm.at[late], sem.at[2]))
     copies[-1].start()
@@ -247,7 +265,7 @@
                 pltpu.VMEM((rows, d_local), bf),
                 pltpu.VMEM((rows - RB, d_local), bf),
                 pltpu.VMEM((RB, d_local), f32),
-                pltpu.VMEM((RB, LANES), f32),
+                pltpu.VMEM((8, RB), f32),
                 pltpu.VMEM((1, d_local), f32),
             ),
             in_specs=[hbm] * 4,
@@ -263,7 +281,7 @@
                 pltpu.VMEM((nrb, RB, LANES), f32),
                 pltpu.VMEM((nrb, 8, RB), f32),
                 pltpu.VMEM((nrb, n_tp - 1, 8, RB), f32),
-                dma((2,)), dma((WSEM,)), dma, dma,
+                dma((2,)), dma((CN // LANES,)), dma((WSEM,)), dma, dma,
                 dma, dma, dma((nch, nrb)), dma, dma((nrb,)), dma((nrb,)),
             ],
             compiler_params=pltpu.CompilerParams(
@@ -275,7 +293,7 @@
             out_shape=(out, out),
             in_specs=[vmem] * 5,
             out_specs=(hbm, hbm),
-            scratch_shapes=[pltpu.VMEM((RB, d_local), bf), dma((3,))],
+            scratch_shapes=[pltpu.VMEM((RB, d_local), bf), pltpu.VMEM((RB, LANES), f32), dma((3,))],
             compiler_params=pltpu.CompilerParams(vmem_limit_bytes=4 * 1024 * 1024),
         )(*parts)
 

time: 56.2 us -> 54.7 us (0.973)
  Pallas kernels: 55.4 us -> 54 us
    pallas_call x1, Pallas kernels: 54.1 us -> 52.6 us  [local_step(): pl.pallas_call(functools.partial(main_kernel, n_tp), out_shape=(pltpu.VME...]
where the time goes in v4:
time: 54.7 us; the launch traced here: 54.6 us
  Pallas kernels  54 us (99%)
  between operations  0.64 us (1%)
    pallas_call x1, Pallas kernels, local_step(): pl.pallas_call(functools.partial(main_kernel, n_tp), out_shape=(pltpu.VME...  52.6 us
    pallas_call x1, Pallas kernels, local_step(): pl.pallas_call(finish_kernel, out_shape=(out, out), in_specs=[vmem] * 5,...  1.34 us

profile of v4, /device:TPU:0, one launch (start us, length us, event | category | flops | bytes accessed | tf_op | source)
XLA Modules:
  0.0 54.6 jit_solution(13618567784144505551)
XLA Ops:
  0.6 52.6 %shard_map.59 = (bf16[256,2048]{1,0:T(8,128)(2,1)S(1)}, bf16[128,2048]{1,0:T(8,128)(2,1)S(1)}, f32[128,2048]{1,0:T(8,128)S(1)}, f32[8,128]{1,0:T(8,128)S(1)}, f32[1,2048]{1,0:T(1,128)S(1)}) custom-call(bf16[256,2048]{1,0:T(8,128)(2,1)} %a_hbm.1, bf16[2048,8192]{1,0:T(8,128)(2,1)} %w_hbm.1, bf16[256,2048]{1,0:T(8,128)(2,1)} %r_hbm.1, f32[1,2048]{1,0:T(1,128)} %bitcast.1), custom_call_target="tpu_custom_call" | custom-call | tf_op jit(solution)/shard_map/pallas_call | solution.py:262
  53.3 1.3 %shard_map.60 = (bf16[256,2048]{1,0:T(8,128)(2,1)}, bf16[256,2048]{1,0:T(8,128)(2,1)}) custom-call(bf16[256,2048]{1,0:T(8,128)(2,1)S(1)} %get-tuple-element.7.hid_ref, bf16[128,2048]{1,0:T(8,128)(2,1)S(1)} %get-tuple-element.8.nrm_ref, f32[128,2048]{1,0:T(8,128)S(1)} %get-tuple-element.9.last_ref, f32[8,128]{1,0:T(8,128)S(1)} %get-tuple-element.10.scale_ref, ...), custom_call_target="tpu_custom_call" | custom-call | tf_op jit(solution)/shard_map/pallas_call | solution.py:291

commit v5 on v4

v5 whole, which is shorter than its diff:
```python
import functools

import jax
import jax.numpy as jnp
from jax import lax
from jax.experimental import pallas as pl
from jax.experimental.pallas import tpu as pltpu
from jax.sharding import PartitionSpec as P

EPS = 1e-5
CN = 256
RB = 128
DEPTH = 4
WSEM = 4
LANES = 128
MESH = pl.DeviceIdType.MESH


def fold(x):
    s = x[:, :LANES]
    for k in range(1, x.shape[1] // LANES):
        s = s + x[:, k * LANES:(k + 1) * LANES]
    return s


def spread(inv):
    return jnp.broadcast_to(inv[0:1], (LANES, inv.shape[1])).T


def main_kernel(n_tp, a_hbm, w_hbm, r_hbm, g_hbm,
                hid_ref, nrm_ref, last_ref, scale_ref, gain,
                a, w, res, sbuf, own, rbuf, sq, st_out, st_in,
                head_sem, late_sem, w_sem, send_sem, far_sem, part_sem, sst_sem, rst_sem):
    rows, d_local = hid_ref.shape
    d_model = d_local * n_tp
    nch = d_local // CN
    nrb = rows // RB
    half = 2 * nch
    last = nrb - 1
    bf, f32 = jnp.bfloat16, jnp.float32

    me = lax.axis_index("tp")
    chip = me // 2
    core = me % 2
    partner = chip * 2 + (1 - core)
    far = (1 - chip) * 2

    def dev(t):
        return {"tp": t}

    def block(b):
        return pl.ds(b * RB, RB)

    def wait(ref, sem):
        pltpu.make_async_copy(ref, ref, sem).wait()

    def w_pair(j, act):
        is_far = jnp.int32(j < nch)
        k = j - nch
        is_part = jnp.int32(k < nch // 2) * (1 - is_far)
        is_own = 1 - is_far - is_part
        near = is_part * partner + is_own * me
        base = is_far * (far * nch + j) + (1 - is_far) * (near * nch + 2 * (k - is_own * (nch // 2)))
        step = is_far * nch + (1 - is_far)
        for p in range(2):
            col = pl.multiple_of((base + p * step) * CN, CN)
            act(pltpu.make_async_copy(w_hbm.at[:, pl.ds(col, CN)], w.at[2 * j + p], w_sem.at[j % WSEM]))

    def w_start(j):
        w_pair(j, lambda c: c.start())

    def w_wait(j):
        wait(w.at[pl.ds(2 * j, 2)], w_sem.at[j % WSEM])

    hc = CN // 2

    def w_piece(p):
        col = pl.multiple_of(far * d_local + p * hc, hc)
        return pltpu.make_async_copy(w_hbm.at[:, pl.ds(col, hc)], w.at[0, :, pl.ds(p * hc, hc)], head_sem.at[1 + p])

    def w_second():
        col = pl.multiple_of((far + 1) * d_local, CN)
        return pltpu.make_async_copy(w_hbm.at[:, pl.ds(col, CN)], w.at[1], w_sem.at[0])

    def far_send(i, b):
        return pltpu.make_async_remote_copy(
            src_ref=sbuf.at[i, block(b), :], dst_ref=rbuf.at[1 + core, i // 2, block(b), :],
            send_sem=send_sem, recv_sem=far_sem.at[group_of(i // 2, b)],
            device_id=dev(far + i % 2), device_id_type=MESH)

    quarter = nch // 2

    def group_of(c, b):
        if b < last:
            return b * 2 + c // quarter
        g = last * 2
        if isinstance(c, int):
            return g + (0 if c < quarter else 1 if c < nch - 2 else c - (nch - 2) + 2)
        return g + jnp.int32(c >= quarter) + jnp.int32(c >= nch - 2) + jnp.int32(c >= nch - 1)

    def groups(b):
        if b < last:
            return [(0, quarter), (quarter, nch)]
        return [(0, quarter), (quarter, nch - 2), (nch - 2, nch - 1), (nch - 1, nch)]

    a_top, a_bot = (pltpu.make_async_copy(a_hbm.at[pl.ds(k * RB, RB * (1 if k == 0 else nrb - 1))],
                                          a.at[pl.ds(k * RB, RB * (1 if k == 0 else nrb - 1))],
                                          head_sem.at[0] if k == 0 else late_sem) for k in range(2))
    r_copy = pltpu.make_async_copy(r_hbm, res, late_sem)
    g_copy = pltpu.make_async_copy(g_hbm, gain, late_sem)

    barrier = pltpu.get_barrier_semaphore()
    for k in range(1, n_tp):
        pl.semaphore_signal(barrier, inc=1, device_id=dev((me + k) % n_tp), device_id_type=MESH)
    a_top.start()
    w_piece(0).start()
    w_piece(1).start()

    def top_product(i):
        sbuf[i, :RB] = jnp.dot(a[:RB], w[i], preferred_element_type=f32).astype(bf)

    with jax.named_scope("a_wait"):
        a_top.wait()
    w_second().start()

    def piece_send(p):
        cols = pl.ds(p * hc, hc)
        pltpu.make_async_remote_copy(
            src_ref=sbuf.at[0, block(0), cols], dst_ref=rbuf.at[1 + core, 0, block(0), cols],
            send_sem=send_sem, recv_sem=far_sem.at[group_of(0, 0)], device_id=dev(far), device_id_type=MESH).start()

    for p in range(2):
        cols = pl.ds(p * hc, hc)
        w_piece(p).wait()
        with jax.named_scope(f"first{p}"):
            sbuf[0, :RB, cols] = jnp.dot(a[:RB], w[0, :, cols], preferred_element_type=f32).astype(bf)
        if p == 0:
            w_start(1)
            with jax.named_scope("barrier_wait"):
                pl.semaphore_wait(barrier, n_tp - 1)

            @pl.when(core == 0)
            def _():
                piece_send(0)
        else:
            @pl.when(core == 1)
            def _():
                piece_send(0)

            piece_send(1)
    for j in range(2, DEPTH):
        w_start(j)
    wait(w.at[1], w_sem.at[0])
    with jax.named_scope("far_product"):
        top_product(1)
    far_send(1, 0).start()

    @pl.loop(1, nch)
    def _(j):
        w_start(j + DEPTH - 1)
        w_wait(j)
        for p in range(2):
            with jax.named_scope("far_product"):
                top_product(2 * j + p)
            far_send(2 * j + p, 0).start()

    a_bot.start()
    r_copy.start()
    g_copy.start()
    a_bot.wait()
    r_copy.wait()
    g_copy.wait()

    @pl.loop(0, half)
    def _(i):
        with jax.named_scope("bot_product"):
            sbuf[i, RB:] = jnp.dot(a[RB:], w[i], preferred_element_type=f32).astype(bf)

    def near_loop(first, body):
        @pl.loop(0, nch // 2)
        def _(k):
            j = first + k

            @pl.when(j + DEPTH - 1 < 2 * nch)
            def _():
                w_start(j + DEPTH - 1)

            w_wait(j)
            for p in range(2):
                with jax.named_scope("near_product"):
                    body(2 * k + p, jnp.dot(a[...], w[2 * j + p], preferred_element_type=f32))

    def to_partner(c, x):
        sbuf[half + c] = x.astype(bf)
        pltpu.make_async_remote_copy(
            src_ref=sbuf.at[half + c], dst_ref=rbuf.at[0, c], send_sem=send_sem, recv_sem=part_sem,
            device_id=dev(partner), device_id_type=MESH).start()

    def keep(c, x):
        cols = pl.ds(pl.multiple_of(c * CN, CN), CN)
        own[c] = x + res[:, cols].astype(f32)

    near_loop(nch, to_partner)
    near_loop(nch + nch // 2, keep)
    wait(rbuf.at[0], part_sem)

    @pl.loop(0, nch)
    def _(c):
        own[c] = own[c] + rbuf[0, c].astype(f32)

    def issue(b, lo, hi):
        if 1 <= b < nrb:
            for c in range(lo, hi):
                far_send(2 * c, b).start()
                far_send(2 * c + 1, b).start()

    def add_chunk(b, c):
        cols = pl.ds(c * CN, CN)
        rs = block(b)
        h = own[c, rs, :] + (rbuf[1, c, rs, :].astype(f32) + rbuf[2, c, rs, :].astype(f32))
        hid_ref[rs, cols] = h.astype(bf)
        if b == last:
            last_ref[:, cols] = h
        else:
            own[c, rs, :] = h
        s = fold(h * h)
        sq[b] = s if c == 0 else sq[b] + s

    def stat_copy(b, k):
        return pltpu.make_async_remote_copy(
            src_ref=st_out.at[b], dst_ref=st_in.at[b, k - 1], send_sem=sst_sem,
            recv_sem=rst_sem.at[b], device_id=dev((me + k) % n_tp), device_id_type=MESH)

    def send_stats(b):
        with jax.named_scope(f"send_stats{b}"):
            t = jnp.sum(sq[b].T, axis=0, keepdims=True)
            st_out[b] = jnp.broadcast_to(t, (8, RB))
            for k in (2, 3, 1):
                stat_copy(b, k).start()

    def scale(b):
        with jax.named_scope(f"stat_wait{b}"):
            wait(st_in.at[b], rst_sem.at[b])
        t = st_out[b] + st_in[b, 0] + st_in[b, 1] + st_in[b, 2]
        return lax.rsqrt(t / d_model + EPS)

    def normalise(b):
        sq[b] = spread(scale(b))

        @pl.loop(0, nch)
        def _(c):
            for k in range(CN // LANES):
                cols = pl.ds(pl.multiple_of(c * CN + k * LANES, LANES), LANES)
                v = own[c, block(b), k * LANES:(k + 1) * LANES] * sq[b] * gain[:, cols]
                nrm_ref[block(b), cols] = v.astype(bf)

    for b in range(nrb):
        for n, (lo, hi) in enumerate(groups(b)):
            if b > 0 and n == 2:
                normalise(b - 1)
            with jax.named_scope(f"far_wait{b}_{n}"):
                wait(rbuf.at[pl.ds(1, 2), pl.ds(lo, hi - lo), block(b), :], far_sem.at[group_of(lo, b)])
            if n == 0:
                issue(b + 1, 0, quarter)
            for c in range(lo, hi):
                add_chunk(b, c)
        send_stats(b)
        issue(b + 1, quarter, nch)

    with jax.named_scope("drain"):
        wait(sbuf, send_sem)
    scale_ref[...] = scale(last)
    with jax.named_scope("drain2"):
        wait(st_in, sst_sem)


def finish_kernel(hid_ref, nrm_ref, last_ref, scale_ref, gain_ref, hid_hbm, nrm_hbm, buf, scale, sem):
    rows, d_local = hid_hbm.shape
    early = nrm_ref.shape[0]
    late = pl.ds(early, rows - early)
    copies = [
        pltpu.make_async_copy(hid_ref, hid_hbm, sem.at[0]),
        pltpu.make_async_copy(nrm_ref, nrm_hbm.at[pl.ds(0, early)], sem.at[1]),
    ]
    for c in copies:
        c.start()

    scale[...] = spread(scale_ref[...])

    @pl.loop(0, d_local // LANES)
    def _(j):
        cols = pl.ds(pl.multiple_of(j * LANES, LANES), LANES)
        buf[:, cols] = (last_ref[:, cols] * scale[...] * gain_ref[:, cols]).astype(jnp.bfloat16)

    copies.append(pltpu.make_async_copy(buf, nrm_hbm.at[late], sem.at[2]))
    copies[-1].start()
    for c in copies:
        c.wait()


def solution(mesh):
    n_tp = mesh.shape["tp"]

    def local_step(attn_blk, w_blk, resid_blk, gain_blk):
        rows, depth = attn_blk.shape
        d_local = resid_blk.shape[1]
        nch = d_local // CN
        nrb = rows // RB
        bf, f32 = jnp.bfloat16, jnp.float32
        dma = pltpu.SemaphoreType.DMA
        vmem = pl.BlockSpec(memory_space=pltpu.VMEM)
        hbm = pl.BlockSpec(memory_space=pl.ANY)
        parts = pl.pallas_call(
            functools.partial(main_kernel, n_tp),
            out_shape=(
                pltpu.VMEM((rows, d_local), bf),
                pltpu.VMEM((rows - RB, d_local), bf),
                pltpu.VMEM((RB, d_local), f32),
                pltpu.VMEM((8, RB), f32),
                pltpu.VMEM((1, d_local), f32),
            ),
            in_specs=[hbm] * 4,
            out_specs=(vmem,) * 5,
            scratch_shapes=[
                pltpu.VMEM((rows, depth), bf),
                pltpu.VMEM((4 * nch, depth, CN), bf),
                pltpu.VMEM((rows, d_local), bf),
                pltpu.VMEM((3 * nch, rows, CN), bf),
                pltpu.VMEM((nch, rows, CN), f32),
                pltpu.VMEM((3, nch, rows, CN), bf),
                pltpu.VMEM((nrb, RB, LANES), f32),
                pltpu.VMEM((nrb, 8, RB), f32),
                pltpu.VMEM((nrb, n_tp - 1, 8, RB), f32),
                dma((3,)), dma, dma((WSEM,)), dma, dma((2 * nrb + 2,)), dma, dma, dma((nrb,)),
            ],
            compiler_params=pltpu.CompilerParams(
                collective_id=0, has_side_effects=True, vmem_limit_bytes=54 * 1024 * 1024),
        )(attn_blk, w_blk, resid_blk, gain_blk.reshape(1, d_local))
        out = jax.ShapeDtypeStruct((rows, d_local), bf)
        return pl.pallas_call(
            finish_kernel,
            out_shape=(out, out),
            in_specs=[vmem] * 5,
            out_specs=(hbm, hbm),
            scratch_shapes=[pltpu.VMEM((RB, d_local), bf), pltpu.VMEM((RB, LANES), f32), dma((3,))],
            compiler_params=pltpu.CompilerParams(vmem_limit_bytes=4 * 1024 * 1024),
        )(*parts)

    return jax.shard_map(
        local_step,
        mesh=mesh,
        in_specs=(P("data", "tp"), P("tp", None), P("data", "tp"), P("tp")),
        out_specs=(P("data", "tp"), P("data", "tp")),
        check_vma=False,
    )
```

time: 54.7 us -> 54.8 us (level)
  no operation moved by 1% of the time
where the time goes in v5:
time: 54.8 us; the launch traced here: 54.7 us
  Pallas kernels  54.1 us (99%)
  between operations  0.64 us (1%)
    pallas_call x1, Pallas kernels, local_step(): pl.pallas_call(functools.partial(main_kernel, n_tp), out_shape=(pltpu.VME...  52.7 us
    pallas_call x1, Pallas kernels, local_step(): pl.pallas_call(finish_kernel, out_shape=(out, out), in_specs=[vmem] * 5,...  1.34 us

profile of v5, /device:TPU:0, one launch (start us, length us, event | category | flops | bytes accessed | tf_op | source)
XLA Modules:
  0.0 54.7 jit_solution(15573841789215407448)
XLA Ops:
  0.6 52.7 %shard_map.59 = (bf16[256,2048]{1,0:T(8,128)(2,1)S(1)}, bf16[128,2048]{1,0:T(8,128)(2,1)S(1)}, f32[128,2048]{1,0:T(8,128)S(1)}, f32[8,128]{1,0:T(8,128)S(1)}, f32[1,2048]{1,0:T(1,128)S(1)}) custom-call(bf16[256,2048]{1,0:T(8,128)(2,1)} %a_hbm.1, bf16[2048,8192]{1,0:T(8,128)(2,1)} %w_hbm.1, bf16[256,2048]{1,0:T(8,128)(2,1)} %r_hbm.1, f32[1,2048]{1,0:T(1,128)} %bitcast.1), custom_call_target="tpu_custom_call" | custom-call | tf_op jit(solution)/shard_map/pallas_call | solution.py:313
  53.4 1.3 %shard_map.60 = (bf16[256,2048]{1,0:T(8,128)(2,1)}, bf16[256,2048]{1,0:T(8,128)(2,1)}) custom-call(bf16[256,2048]{1,0:T(8,128)(2,1)S(1)} %get-tuple-element.7.hid_ref, bf16[128,2048]{1,0:T(8,128)(2,1)S(1)} %get-tuple-element.8.nrm_ref, f32[128,2048]{1,0:T(8,128)S(1)} %get-tuple-element.9.last_ref, f32[8,128]{1,0:T(8,128)S(1)} %get-tuple-element.10.scale_ref, ...), custom_call_target="tpu_custom_call" | custom-call | tf_op jit(solution)/shard_map/pallas_call | solution.py:340
